TPU v7x, 32 devices: a whole 2x2x4 slice. The times are simulated.
32 devices in a mesh: grp: 2 (over core), tile: 16 (over z, y, x).
Axes of the slice: x: 2, y: 2, z: 4, core: 2. Of those that a mesh axis runs over, the one named last changes fastest.
Arguments:
- attn_input: bfloat16 [2048, 4096], P(('grp', 'tile')), may hold values from -9 to 9
- mlp_input: bfloat16 [2048, 4096], P(('grp', 'tile')), may hold values from -9 to 9
Outputs:
- hess_attn: float32 [16, 1024, 1024], P('tile', 'grp')
- hess_mlp: float32 [16, 1024, 1024], P('tile', 'grp')
All inputs are finite; a program needn't handle non-finite values.
Results may differ from a plain program's by a relative error of at most 0.0003.
Values may be sent and summed in bfloat16 or wider, within the bound.
A program may use at most 192 MiB of HBM per device.

v0:
```python
import jax
import jax.numpy as jnp
from jax import lax
from jax.experimental import pallas as pl
from jax.experimental.pallas import tpu as pltpu
from jax.sharding import PartitionSpec as P

ROWB = 4
TOKB = 32
MESH = pl.DeviceIdType.MESH
END_HOP = 2
MID_HOP = 4


def tile_first(inputs, tile_count):
    tok_rows, feat_width = inputs.shape
    col_blocks = tile_count // ROWB
    row_width = feat_width // ROWB
    col_width = feat_width // col_blocks

    def accumulate(turn_idx, partial_value):
        tok_block = lax.dynamic_slice_in_dim(inputs, turn_idx * TOKB, TOKB, 0)
        row_parts = tok_block.reshape(TOKB, ROWB, row_width).transpose(1, 0, 2)
        row_send = jnp.repeat(row_parts, col_blocks, axis=0)
        col_parts = tok_block.reshape(TOKB, col_blocks, col_width).transpose(1, 0, 2)
        col_send = jnp.tile(col_parts, (ROWB, 1, 1))
        rows_in, cols_in = (
            lax.all_to_all(row_send, "tile", split_axis=0, concat_axis=0, tiled=True),
            lax.all_to_all(col_send, "tile", split_axis=0, concat_axis=0, tiled=True),
        )
        rows_flat = rows_in.reshape(tile_count * TOKB, row_width)
        cols_flat = cols_in.reshape(tile_count * TOKB, col_width)
        return partial_value + lax.dot_general(
            rows_flat, cols_flat, (((0,), (0,)), ((), ())), preferred_element_type=jnp.float32
        )

    partial_value = lax.fori_loop(
        0, tok_rows // TOKB, accumulate, jnp.zeros((row_width, col_width), jnp.float32)
    )
    shares = lax.psum_scatter(partial_value, "grp", scatter_dimension=0, tiled=True)
    return shares[None]


def hessian_share(inputs):
    tile_count = lax.axis_size("tile")
    group_count = lax.axis_size("grp")
    norm_factor = 2.0 / (inputs.shape[0] * tile_count * group_count)
    shares = tile_first(inputs, tile_count)
    return shares * norm_factor


def ring_place(member):
    return member + (member // 2) * (1 - 2 * (member % 2))


def piece_of(home, turn):
    near = home + 1 - 2 * (home % 2)
    far = (home + 2) % ROWB
    return jnp.where(turn == 0, home, jnp.where(turn == 1, near, jnp.where(turn == 2, far, ROWB - 1 - home)))


def kernel(xa, xm, out_a, out_m, cbuf, dbuf, rbuf, c_recv, d_recv, r_recv, s1_send, dn_send, up_send, d_send, r_send):
    lines = planes = ROWB
    g = lax.axis_index("grp")
    t = lax.axis_index("tile")
    z, p = t // planes, t % planes
    tok, _ = xa.shape
    ct = cbuf.shape[-1]
    rh = rbuf.shape[-1]
    xs = (xa, xm)
    outs = (out_a, out_m)
    half = pl.ds(pl.multiple_of(g * rh, rh), rh)

    fwd = (ring_place(p) - ring_place(z) + planes) % planes
    bwd = (planes - fwd) % planes
    is_root = fwd == 0
    ring_fwd = ring_place((ring_place(p) + 1) % planes)
    ring_bwd = ring_place((ring_place(p) + planes - 1) % planes)

    def chip(zz, pp, gg=None):
        return (g if gg is None else gg, zz * planes + pp)

    barrier = pltpu.get_barrier_semaphore()
    pl.semaphore_signal(barrier, inc=1, device_id=chip(z, p, 1 - g), device_id_type=MESH)
    for turn in range(1, planes):
        pl.semaphore_signal(barrier, inc=1, device_id=chip(z, piece_of(p, turn)), device_id_type=MESH)

    @pl.when(z > 0)
    def _():
        pl.semaphore_signal(barrier, inc=1, device_id=chip(z - 1, p), device_id_type=MESH)

    @pl.when(z < lines - 1)
    def _():
        pl.semaphore_signal(barrier, inc=1, device_id=chip(z + 1, p), device_id_type=MESH)

    pl.semaphore_wait(barrier, planes + jnp.where(z > 0, 1, 0) + jnp.where(z < lines - 1, 1, 0))

    def s1_copy(a, turn):
        other = piece_of(p, turn)
        cols = pl.ds(pl.multiple_of(other * ct, ct), ct)
        return pltpu.make_async_remote_copy(
            src_ref=xs[a].at[:, cols], dst_ref=cbuf.at[a, z, p], send_sem=s1_send.at[a, turn - 1],
            recv_sem=c_recv.at[a, z, p], device_id=chip(z, other), device_id_type=MESH)

    def own_copy(a):
        cols = pl.ds(pl.multiple_of(p * ct, ct), ct)
        return pltpu.make_async_copy(xs[a].at[:, cols], cbuf.at[a, z, p], c_recv.at[a, z, p])

    def line_copy(a, slot, piece, down):
        return pltpu.make_async_remote_copy(
            src_ref=cbuf.at[a, slot, piece], dst_ref=cbuf.at[a, slot, piece],
            send_sem=(dn_send if down else up_send).at[a, slot, piece], recv_sem=c_recv.at[a, slot, piece],
            device_id=chip(z - 1 if down else z + 1, p), device_id_type=MESH)

    def pair_copy(a, slot, piece):
        return pltpu.make_async_remote_copy(
            src_ref=cbuf.at[a, slot, piece], dst_ref=dbuf.at[a, slot, piece], send_sem=d_send.at[a, slot, piece],
            recv_sem=d_recv.at[a, slot, piece], device_id=chip(z, p, 1 - g), device_id_type=MESH)

    def ring_copy(src, a, slot, gg, piece, way):
        return pltpu.make_async_remote_copy(
            src_ref=src, dst_ref=rbuf.at[a, slot, gg, piece], send_sem=r_send.at[a, slot, gg, piece],
            recv_sem=r_recv.at[a, slot, gg, piece],
            device_id=chip(z, ring_fwd * (1 - way) + ring_bwd * way), device_id_type=MESH)

    def landed(ref, sem):
        pltpu.make_async_copy(ref, ref, sem).wait()

    for a in range(2):
        own_copy(a).start()
    for turn in range(1, planes):
        for a in range(2):
            s1_copy(a, turn).start()
    for out in outs:
        out[...] = jnp.zeros_like(out)

    def root_feed(src, a, slot, gg, piece, turn):
        @pl.when(is_root)
        def _():
            pltpu.make_async_copy(src, rbuf.at[a, slot, gg, piece], r_recv.at[a, slot, gg, piece]).start()
            ring_copy(src, a, slot, gg, piece, (turn + gg) % 2).start()

    def each_slot(k, action):
        dist, turn, a = k // (2 * planes), (k // 2) % planes, k % 2
        high, low = z + dist, z - dist

        @pl.when((k >= 0) & (k < 2 * planes * lines))
        def _():
            @pl.when(high < lines)
            def _():
                action(a, high, turn, dist, True)

            @pl.when((dist > 0) & (low >= 0))
            def _():
                action(a, low, turn, dist, False)

    def col_phase(a, slot, turn, dist, from_high):
        piece = piece_of(p, turn)
        landed(cbuf.at[a, slot, piece], c_recv.at[a, slot, piece])
        if from_high:
            @pl.when(z > 0)
            def _():
                line_copy(a, slot, piece, True).start()

            @pl.when((dist == 0) & (z < lines - 1))
            def _():
                line_copy(a, slot, piece, False).start()
        else:
            @pl.when(z < lines - 1)
            def _():
                line_copy(a, slot, piece, False).start()
        pair_copy(a, slot, piece).start()
        root_feed(cbuf.at[a, slot, piece, :, half], a, slot, g, piece, turn)

    def pair_phase(a, slot, turn, dist, from_high):
        piece = piece_of(p, turn)
        landed(dbuf.at[a, slot, piece], d_recv.at[a, slot, piece])
        root_feed(dbuf.at[a, slot, piece, :, half], a, slot, 1 - g, piece, turn)

    def row_phase(way, span):
        def action(a, slot, turn, dist, from_high):
            piece = piece_of(z, turn)
            gg = (turn + way) % 2
            landed(rbuf.at[a, slot, gg, piece], r_recv.at[a, slot, gg, piece])

            @pl.when((span > 0) & (span < planes - 1))
            def _():
                ring_copy(rbuf.at[a, slot, gg, piece], a, slot, gg, piece, way).start()

        return action

    def multiply(a, slot, turn, dist, from_high):
        @pl.when(turn == planes - 1)
        def _():
            for arr in range(2):
                @pl.when(a == arr)
                def _():
                    total = outs[arr]
                    for cols, gg in ((cbuf, g), (dbuf, 1 - g)):
                        total[...] += lax.dot_general(
                            rbuf[arr, slot, gg].reshape(planes * tok, rh),
                            cols[arr, slot].reshape(planes * tok, ct),
                            (((0,), (0,)), ((), ())), preferred_element_type=jnp.float32)

    hop = jnp.where((z == 0) | (z == lines - 1), END_HOP, MID_HOP)
    last = 1 + hop * (planes - 1)

    def step(k, carry):
        each_slot(k, col_phase)
        each_slot(k - 1, pair_phase)
        each_slot(k - 1 - hop * jnp.where(fwd == 0, 1, fwd), row_phase(0, fwd))
        each_slot(k - 1 - hop * jnp.where(bwd == 0, 1, bwd), row_phase(1, bwd))
        each_slot(k - last, multiply)
        return carry

    lax.fori_loop(0, 2 * planes * lines + last, step, 0)

    for a in range(2):
        for turn in range(1, planes):
            s1_copy(a, turn).wait_send()

    def finish(a, slot, turn, dist, from_high):
        piece = piece_of(p, turn)
        if from_high:
            @pl.when(z > 0)
            def _():
                line_copy(a, slot, piece, True).wait_send()

            @pl.when((dist == 0) & (z < lines - 1))
            def _():
                line_copy(a, slot, piece, False).wait_send()
        else:
            @pl.when(z < lines - 1)
            def _():
                line_copy(a, slot, piece, False).wait_send()
        pair_copy(a, slot, piece).wait_send()
        row_piece = piece_of(z, turn)
        for gg in range(2):
            way = (turn + gg) % 2
            span = fwd * (1 - way) + bwd * way

            @pl.when(span < planes - 1)
            def _():
                ring_copy(rbuf.at[a, slot, gg, row_piece], a, slot, gg, row_piece, way).wait_send()

    def finish_step(k, carry):
        each_slot(k, finish)
        return carry

    lax.fori_loop(0, 2 * planes * lines, finish_step, 0)


def fused(attn_input, mlp_input):
    groups, tiles = lax.axis_size("grp"), lax.axis_size("tile")
    tok, width = attn_input.shape
    ct, rh = width // ROWB, width // ROWB // groups
    norm_factor = 2.0 / (tok * tiles * groups)
    dma = pltpu.SemaphoreType.DMA
    cell = (2, ROWB, ROWB)
    hess = pl.pallas_call(
        kernel,
        out_shape=[jax.ShapeDtypeStruct((rh, ct), jnp.float32)] * 2,
        in_specs=[pl.BlockSpec(memory_space=pl.ANY)] * 2,
        out_specs=[pl.BlockSpec(memory_space=pltpu.VMEM)] * 2,
        scratch_shapes=[
            pltpu.VMEM(cell + (tok, ct), jnp.bfloat16),
            pltpu.VMEM(cell + (tok, ct), jnp.bfloat16),
            pltpu.VMEM((2, ROWB, groups, ROWB, tok, rh), jnp.bfloat16),
            dma(cell), dma(cell), dma((2, ROWB, groups, ROWB)),
            dma((2, ROWB - 1)), dma(cell), dma(cell), dma(cell), dma((2, ROWB, groups, ROWB)),
        ],
        compiler_params=pltpu.CompilerParams(collective_id=0, has_side_effects=True, vmem_limit_bytes=48 * 1024 * 1024),
    )(attn_input, mlp_input)
    return hess[0][None] * norm_factor, hess[1][None] * norm_factor


def body(attn_input, mlp_input):
    if lax.axis_size("grp") == 2 and lax.axis_size("tile") == ROWB * ROWB:
        return fused(attn_input, mlp_input)
    return (hessian_share(attn_input), hessian_share(mlp_input))


def solution(mesh):
    in_specs = (P(("grp", "tile"), None), P(("grp", "tile"), None))
    out_specs = (P("tile", "grp", None), P("tile", "grp", None))
    return jax.shard_map(body, mesh=mesh, in_specs=in_specs, out_specs=out_specs, check_vma=False)
```

profile of v0, /device:TPU:3, one launch (start us, length us, event | category | flops | bytes accessed | tf_op | source)
XLA Modules:
  0.0 93.3 jit_solution(15932997600308177860)
XLA Ops:
  0.6 0.0 copy-start
  0.6 1.0 %copy-done = bf16[64,4096]{1,0:T(8,128)(2,1)S(1)} copy-done((bf16[64,4096]{1,0:T(8,128)(2,1)S(1)}, bf16[64,4096]{1,0:T(8,128)(2,1)}, u32[]{:S(2)}) %copy-start) | copy-done | bytes 524312
  1.7 0.0 copy-start.1
  1.7 1.0 %copy-done.1 = bf16[64,4096]{1,0:T(8,128)(2,1)S(1)} copy-done((bf16[64,4096]{1,0:T(8,128)(2,1)S(1)}, bf16[64,4096]{1,0:T(8,128)(2,1)}, u32[]{:S(2)}) %copy-start.1) | copy-done | bytes 524312
  2.7 87.7 %shard_map.41 = (f32[512,1024]{1,0:T(8,128)S(1)}, f32[512,1024]{1,0:T(8,128)S(1)}) custom-call(bf16[64,4096]{1,0:T(8,128)(2,1)S(1)} %copy-done, bf16[64,4096]{1,0:T(8,128)(2,1)S(1)} %copy-done.1), custom_call_target="tpu_custom_call" | custom-call | tf_op jit(solution)/shard_map/pallas_call | solution.py:260
  90.4 2.9 %multiply_bitcast_fusion = (f32[1,512,1024]{2,1,0:T(8,128)}, f32[1,512,1024]{2,1,0:T(8,128)}) fusion(f32[512,1024]{1,0:T(8,128)S(1)} %get-tuple-element.5, f32[512,1024]{1,0:T(8,128)S(1)} %get-tuple-element.4), kind=kLoop, calls=%fused_computation | loop fusion | flops 1048576 | bytes 8388608 | tf_op jit(solution)/shard_map/mul | solution.py:274
Async XLA Ops:
  0.6 1.0 %copy-start = (bf16[64,4096]{1,0:T(8,128)(2,1)S(1)}, bf16[64,4096]{1,0:T(8,128)(2,1)}, u32[]{:S(2)}) copy-start(bf16[64,4096]{1,0:T(8,128)(2,1)} %xa.1) | copy-start | bytes 1572868
  1.7 1.0 %copy-start.1 = (bf16[64,4096]{1,0:T(8,128)(2,1)S(1)}, bf16[64,4096]{1,0:T(8,128)(2,1)}, u32[]{:S(2)}) copy-start(bf16[64,4096]{1,0:T(8,128)(2,1)} %xm.1) | copy-start | bytes 1572868
where the time goes:
time: 94.7 us; the launch traced here: 93.3 us
  Pallas kernels  87.7 us (93%)
  other arithmetic  2.85 us (3%)
  local copies, waits for them, and re-layouts  2.08 us (2%)
    pallas_call x1, Pallas kernels, fused(): pl.pallas_call(kernel, out_shape=[jax.ShapeDtypeStruct((rh, ct), jnp.floa...  87.7 us
    mul x1, other arithmetic, fused(): return (hess[0][None] * norm_factor, hess[1][None] * norm_factor)  2.85 us
    unnamed x4, local copies, waits for them, and re-layouts  2.08 us

commit v1 on v0

v1 whole, which is shorter than its diff:
```python
import jax
import jax.numpy as jnp
from jax import lax
from jax.experimental import pallas as pl
from jax.experimental.pallas import tpu as pltpu
from jax.sharding import PartitionSpec as P

ROWB = 4
TOKB = 32
MESH = pl.DeviceIdType.MESH
LINE = 0
RING = 1
AHEAD = 3
CROSS_AT = 2
CROSS_LATE = 9
CROSS_WAIT = 5
FAR_LAG = 1
SPAN_LAG = 2
MUL_LAG = 4
VMEM_LIMIT = 48 * 1024 * 1024
IN_SPACE = pltpu.HBM


def tile_first(inputs, tile_count):
    tok_rows, feat_width = inputs.shape
    col_blocks = tile_count // ROWB
    row_width = feat_width // ROWB
    col_width = feat_width // col_blocks

    def accumulate(turn_idx, partial_value):
        tok_block = lax.dynamic_slice_in_dim(inputs, turn_idx * TOKB, TOKB, 0)
        row_parts = tok_block.reshape(TOKB, ROWB, row_width).transpose(1, 0, 2)
        row_send = jnp.repeat(row_parts, col_blocks, axis=0)
        col_parts = tok_block.reshape(TOKB, col_blocks, col_width).transpose(1, 0, 2)
        col_send = jnp.tile(col_parts, (ROWB, 1, 1))
        rows_in, cols_in = (
            lax.all_to_all(row_send, "tile", split_axis=0, concat_axis=0, tiled=True),
            lax.all_to_all(col_send, "tile", split_axis=0, concat_axis=0, tiled=True),
        )
        rows_flat = rows_in.reshape(tile_count * TOKB, row_width)
        cols_flat = cols_in.reshape(tile_count * TOKB, col_width)
        return partial_value + lax.dot_general(
            rows_flat, cols_flat, (((0,), (0,)), ((), ())), preferred_element_type=jnp.float32
        )

    partial_value = lax.fori_loop(
        0, tok_rows // TOKB, accumulate, jnp.zeros((row_width, col_width), jnp.float32)
    )
    shares = lax.psum_scatter(partial_value, "grp", scatter_dimension=0, tiled=True)
    return shares[None]


def hessian_share(inputs):
    tile_count = lax.axis_size("tile")
    group_count = lax.axis_size("grp")
    norm_factor = 2.0 / (inputs.shape[0] * tile_count * group_count)
    shares = tile_first(inputs, tile_count)
    return shares * norm_factor


def ring_place(member):
    return member + (member // 2) * (1 - 2 * (member % 2))


def piece_of(home, turn):
    near = home + 1 - 2 * (home % 2)
    far = (home + 2) % ROWB
    return jnp.where(turn == 0, home, jnp.where(turn == 1, near, jnp.where(turn == 2, far, ROWB - 1 - home)))


def kernel(xa, xm, out_a, out_m, xbuf, cbuf, rbuf, own_sem, ld_sem, x_recv, c_recv, r_recv, s1_send, x_send, d_send, z_send):
    lines = planes = ROWB
    group = 4 * planes
    side = group * (lines - 1)
    total = group * (2 * lines - 1)
    g = lax.axis_index("grp")
    t = lax.axis_index("tile")
    z, p = t // planes, t % planes
    tok, _ = xa.shape
    ct = cbuf.shape[-1]
    rh = ct // 2
    xs = (xa, xm)
    outs = (out_a, out_m)
    is_line = g == LINE
    line_half = pl.ds(LINE * rh, rh)
    my_half = pl.ds(pl.multiple_of(g * rh, rh), rh)

    fwd = (ring_place(p) - ring_place(z) + planes) % planes
    bwd = (planes - fwd) % planes
    is_root = fwd == 0
    ring_fwd = ring_place((ring_place(p) + 1) % planes)
    ring_bwd = ring_place((ring_place(p) + planes - 1) % planes)
    fwd_is_near = ring_fwd == piece_of(p, 1)

    low_side = z < lines // 2
    upper = z // (lines // 2)
    end_z = upper * (lines - 1)
    at_end = z == end_z
    place = p + upper * (planes - 1 - 2 * p)
    beside = 1 + upper * (lines - 3)
    across = end_z + beside - z
    end_step = 2 * upper - 1
    toward = jnp.where(low_side, group, group + side)
    away = group + group + side - toward

    def crosses(turn):
        return (turn >= 1) & (turn <= 2) & ((place == 0) | (place == turn))

    def comes_late(turn, dist):
        return at_end & (dist == 1) & (turn >= 1) & (turn <= 2) & (place == turn)

    slot_late = at_end & ((place == 1) | (place == 2))

    def near_of(turn):
        return turn + 1 - 2 * (turn % 2)

    def far_of(turn):
        return (turn + 2) % planes

    def local_turn(turn):
        return jnp.where(
            is_root, turn, jnp.where(
                z == piece_of(p, 1), near_of(turn), jnp.where(z == piece_of(p, 2), far_of(turn), planes - 1 - turn)))

    def next_turn(turn, way):
        return jnp.where(fwd_is_near == (way == 0), near_of(turn), far_of(turn))

    def chip(zz, pp, gg):
        return (gg, zz * planes + pp)

    pair = chip(z, p, 1 - g)
    ring_next = [chip(z, ring_fwd, RING), chip(z, ring_bwd, RING)]

    def landed(ref, sem):
        pltpu.make_async_copy(ref, ref, sem).wait()

    def cols(block):
        return pl.ds(pl.multiple_of(block * ct, ct), ct)

    def own_index(a, turn, gg):
        return 2 * planes * a + 2 * turn + gg

    def loan_index(a, turn, gg):
        return (2 * gg + a) * (planes - 1) + turn - 1

    def load_own(a):
        return pltpu.make_async_copy(xs[a].at[:, cols(p)], cbuf.at[own_index(a, 0, g)], own_sem.at[a])

    def load(a, turn):
        return pltpu.make_async_copy(
            xs[a].at[:, cols(piece_of(p, turn))], xbuf.at[loan_index(a, turn, g)], ld_sem.at[a, turn - 1])

    for a in range(2):
        load_own(a).start()
    for turn in range(1, planes):
        for a in range(2):
            load(a, turn).start()

    barrier = pltpu.get_barrier_semaphore()

    def greet(device):
        pl.semaphore_signal(barrier, inc=1, device_id=device, device_id_type=MESH)

    greet(pair)

    @pl.when(is_line)
    def _():
        for turn in range(1, planes):
            for gg in range(2):
                greet(chip(z, piece_of(p, turn), gg))
        for turn in range(1, 3):
            @pl.when(crosses(turn))
            def _():
                greet(chip(across, piece_of(p, turn), LINE))

        @pl.when(z > 0)
        def _():
            greet(chip(z - 1, p, LINE))

        @pl.when(z < lines - 1)
        def _():
            greet(chip(z + 1, p, LINE))

        pl.semaphore_wait(
            barrier, planes + jnp.where(z > 0, 1, 0) + jnp.where(z < lines - 1, 1, 0)
            + jnp.where(crosses(1), 1, 0) + jnp.where(crosses(2), 1, 0))

    @pl.when(~is_line)
    def _():
        for device in ring_next:
            greet(device)
        pl.semaphore_wait(barrier, planes + 2)

    def remote(src, dst, send_sem, recv_sem, device):
        return pltpu.make_async_remote_copy(
            src_ref=src, dst_ref=dst, send_sem=send_sem, recv_sem=recv_sem, device_id=device, device_id_type=MESH)

    def s1_copy(a, turn):
        n = own_index(a, turn, g)
        return remote(xbuf.at[loan_index(a, turn, g)], cbuf.at[n], s1_send.at[a, turn - 1], c_recv.at[n],
                      chip(z, piece_of(p, turn), LINE))

    def lend_copy(a, turn):
        n = loan_index(a, turn, RING)
        return remote(xbuf.at[n], xbuf.at[n], x_send.at[a, RING, turn - 1], x_recv.at[a, turn - 1], chip(z, p, LINE))

    def cross_copy(a, turn, gg):
        n = toward + own_index(a, turn, gg)
        return remote(xbuf.at[loan_index(a, turn, gg)], cbuf.at[n], x_send.at[a, gg, turn - 1], c_recv.at[n],
                      chip(end_z, piece_of(p, turn), LINE))

    def line_copy(n, to, zz, sem):
        return remote(cbuf.at[n], cbuf.at[to], sem, c_recv.at[to], chip(zz, p, LINE))

    def pair_copy(n, sem):
        return remote(cbuf.at[n], cbuf.at[n], sem, c_recv.at[n], pair)

    def ring_copy(buf, n, to, way, sem):
        return remote(buf.at[n], rbuf.at[to], sem, r_recv.at[to], ring_next[way])

    def share_copy(n, sem):
        rows = rbuf.at[n, :, line_half]
        return remote(rows, rows, sem, r_recv.at[n], pair)

    def spot(dist, near):
        from_high = low_side == near
        inside = jnp.where(from_high, z + dist < lines, z >= dist)
        sd = jnp.where((dist == 0) | from_high, dist, dist + lines - 1)
        return sd, inside & (dist < lines)

    def drain(count, sem, buf):
        ref = buf.at[pl.ds(0, count)]
        pltpu.make_async_copy(ref, ref, sem).wait()

    def col_turn(sd, turn, dist, near):
        for a in range(2):
            for gg in (LINE, RING):
                n = group * sd + own_index(a, turn, gg)

                def one(n=n, gg=gg):
                    landed(cbuf.at[n], c_recv.at[n])
                    if near is None or near is False:
                        main_ok = True
                    else:
                        main_ok = ~at_end
                    if dist is None:
                        if turn in (1, 2):
                            main_ok = main_ok & ~crosses(turn)
                        line_copy(n, n + away, z - end_step, z_send.at[2 * lines - 1, turn]).start()
                        to, zz = n + toward, z + end_step
                    else:
                        to, zz = n + group, z + (end_step if near else -end_step)

                    def main():
                        line_copy(n, to, zz, z_send.at[sd, turn]).start()

                    if main_ok is True:
                        main()
                    else:
                        pl.when(main_ok)(main)
                    if not (dist is None and turn == 0 and gg == RING):
                        pair_copy(n, d_send.at[sd, turn]).start()

                if not (dist is None and turn == 0 and gg == LINE):
                    one()

    def feed_turn(sd, turn, dist, near):
        for a in range(2):
            for gg in range(2):
                n = group * sd + own_index(a, turn, gg)
                if not (dist is None and turn == 0 and gg == RING):
                    landed(cbuf.at[n], c_recv.at[n])
                way = (turn + gg) % 2
                to = group * sd + own_index(a, next_turn(turn, way), gg)
                ring_copy(cbuf, n, to, way, z_send.at[sd, turn]).start()

    def row_turn(way, passes):
        def action(sd, turn, dist, near):
            here = local_turn(turn)
            gg = (turn + way) % 2
            n = group * sd + own_index(0, here, gg)
            to = group * sd + own_index(0, next_turn(here, way), gg)
            for a in range(2):
                m, to_m = n + own_index(a, 0, 0), to + own_index(a, 0, 0)
                landed(rbuf.at[m], r_recv.at[m])
                if passes:
                    ring_copy(rbuf, m, to_m, way, z_send.at[sd, turn]).start()
                share_copy(m, d_send.at[sd, turn]).start()

        return action

    def gather_waits(base, skip_own):
        @pl.when(~is_root)
        def _():
            @pl.when(is_line)
            def _():
                for j in range(2 * planes):
                    landed(rbuf.at[base + j, :, line_half], r_recv.at[base + j])

            @pl.when(~is_line)
            def _():
                for j in range(2 * planes):
                    if not (skip_own and j == RING):
                        landed(cbuf.at[base + j], c_recv.at[base + j])

    def product(a, base, count, rows):
        lhs = rows[pl.ds(base, count), :, my_half].reshape(count * tok, rh)
        rhs = cbuf[pl.ds(base, count)].reshape(count * tok, ct)
        outs[a][...] += lax.dot_general(lhs, rhs, (((0,), (0,)), ((), ())), preferred_element_type=jnp.float32)

    def multiply(sd, skip_own=False):
        for a in range(2):
            base = group * sd + own_index(a, 0, 0)
            gather_waits(base, skip_own)

            @pl.when(is_root)
            def _():
                product(a, base, 2 * planes, cbuf)

            @pl.when(~is_root)
            def _():
                product(a, base, 2 * planes, rbuf)

    for a in range(2):
        load_own(a).wait()

        @pl.when(is_line)
        def _():
            n = own_index(a, 0, LINE)

            @pl.when(~at_end)
            def _():
                line_copy(n, n + toward, z + end_step, z_send.at[0, 0]).start()
            line_copy(n, n + away, z - end_step, z_send.at[2 * lines - 1, 0]).start()
            pair_copy(n, d_send.at[0, 0]).start()

        @pl.when(~is_line)
        def _():
            pair_copy(own_index(a, 0, RING), x_send.at[a, LINE, 0]).start()

    for turn in range(1, planes):
        for a in range(2):
            load(a, turn).wait()
            s1_copy(a, turn).start()
    for turn in range(1, 3):
        @pl.when(~is_line & ~at_end & crosses(turn))
        def _():
            for a in range(2):
                lend_copy(a, turn).start()
    for out in outs:
        out[...] = jnp.zeros_like(out)

    def send_cross(a, turn):
        cross_copy(a, turn, LINE).start()
        landed(xbuf.at[loan_index(a, turn, RING)], x_recv.at[a, turn - 1])
        cross_copy(a, turn, RING).start()

    def turns(block, r, shift, action):
        first = r - shift

        @pl.when(block + first // planes == 0)
        def _():
            action(0, first % planes, None, True)

        def along(near, u0, keep):
            dist = block + u0 // planes
            turn = u0 % planes
            sd, inside = spot(dist, near)

            @pl.when(inside & (dist > 0) & keep(dist, turn))
            def _():
                action(sd, turn, dist, near)

        along(True, r - shift + AHEAD, lambda dist, turn: ~at_end | (dist != 1) if turn in (1, 2) else True)
        along(False, r - shift - FAR_LAG + AHEAD, lambda dist, turn: True)
        u_x = planes + 1 + r - shift - CROSS_WAIT
        if u_x % planes in (1, 2):
            late = place == u_x % planes
            along(True, u_x, lambda dist, turn: at_end & (dist == 1) & ~(late & is_col(action)))

    def is_col(action):
        return action is col_turn

    def block_steps(block, carry):
        for r in range(planes):
            @pl.when(is_line)
            def _():
                if r == CROSS_AT % planes:
                    @pl.when((block == CROSS_AT // planes) & ~at_end)
                    def _():
                        for turn in range(1, 3):
                            @pl.when(place == turn)
                            def _():
                                for a in range(2):
                                    send_cross(a, turn)
                if r == CROSS_LATE % planes:
                    @pl.when((block == CROSS_LATE // planes) & ~at_end & (place == 0))
                    def _():
                        for a in range(2):
                            for turn in range(1, 3):
                                send_cross(a, turn)
                turns(block, r, 0, col_turn)

            @pl.when(~is_line & is_root)
            def _():
                turns(block, r, 0, feed_turn)

            @pl.when(~is_line & ~is_root)
            def _():
                @pl.when(fwd < planes - 1)
                def _():
                    turns(block, r, 0, row_turn(0, True))

                @pl.when(bwd < planes - 1)
                def _():
                    turns(block, r, 0, row_turn(1, True))

                @pl.when(fwd == planes - 1)
                def _():
                    turns(block, r, SPAN_LAG, row_turn(0, False))

                @pl.when(bwd == planes - 1)
                def _():
                    turns(block, r, SPAN_LAG, row_turn(1, False))

            at = r - MUL_LAG
            if (at - (planes - 1)) % planes == 0:
                @pl.when(block == (planes - 1 - at) // planes)
                def _():
                    multiply(0, True)
            for near, shift in ((True, 0), (False, FAR_LAG)):
                u0 = at - shift + AHEAD
                if u0 % planes == planes - 1:
                    dist = block + u0 // planes
                    sd, inside = spot(dist, near)

                    @pl.when(inside & (dist > 0) & ~(at_end & (dist == 1)))
                    def _():
                        multiply(sd)
            u0 = planes + 1 + at - CROSS_WAIT
            if u0 % planes == 2:
                @pl.when(at_end & ~slot_late & (block + u0 // planes == 1))
                def _():
                    multiply(toward // group)
        return carry

    steps = planes * lines - AHEAD + FAR_LAG + MUL_LAG
    lax.fori_loop(0, (steps + planes - 1) // planes, block_steps, 0)

    @pl.when(slot_late)
    def _():
        for a in range(2):
            @pl.when(is_line)
            def _():
                for gg in (LINE, RING):
                    n = toward + own_index(a, place, gg)
                    landed(cbuf.at[n], c_recv.at[n])
                    pair_copy(n, d_send.at[toward // group, place]).start()
        for a in range(2):
            gather_waits(toward + own_index(a, 0, 0), False)
            product(a, toward + own_index(a, 0, 0), 2 * planes, rbuf)

    def done(j, carry):
        dist = j % lines
        near = j < lines
        sd, inside = spot(dist, near)

        @pl.when(inside & (near | (dist > 0)))
        def _():
            for turn in range(planes):
                @pl.when(is_line)
                def _():
                    @pl.when(jnp.logical_not(near) | (~at_end & ~((dist == 0) & crosses(turn))))
                    def _():
                        drain(4, z_send.at[sd, turn], cbuf)

                    @pl.when(dist == 0)
                    def _():
                        drain(4, z_send.at[2 * lines - 1, turn], cbuf)
                    if turn == 0:
                        @pl.when(dist == 0)
                        def _():
                            drain(2, d_send.at[sd, turn], cbuf)

                        @pl.when(dist > 0)
                        def _():
                            drain(4, d_send.at[sd, turn], cbuf)
                    else:
                        drain(4, d_send.at[sd, turn], cbuf)

                @pl.when(~is_line)
                def _():
                    @pl.when(is_root | (fwd == 2))
                    def _():
                        drain(4, z_send.at[sd, turn], cbuf)

                    @pl.when(~is_root & (fwd != 2))
                    def _():
                        drain(2, z_send.at[sd, turn], cbuf)

                    @pl.when(~is_root)
                    def _():
                        rows = rbuf.at[pl.ds(0, 4), :, line_half]
                        pltpu.make_async_copy(rows, rows, d_send.at[sd, turn]).wait()
        return carry

    lax.fori_loop(0, 2 * lines, done, 0)
    for turn in range(1, planes):
        for a in range(2):
            s1_copy(a, turn).wait_send()
    for a in range(2):
        @pl.when(~is_line)
        def _():
            pair_copy(own_index(a, 0, RING), x_send.at[a, LINE, 0]).wait_send()
        for turn in range(1, 3):
            @pl.when(is_line & ~at_end & crosses(turn))
            def _():
                for gg in range(2):
                    cross_copy(a, turn, gg).wait_send()

            @pl.when(~is_line & ~at_end & crosses(turn))
            def _():
                lend_copy(a, turn).wait_send()


def fused(attn_input, mlp_input):
    groups, tiles = lax.axis_size("grp"), lax.axis_size("tile")
    tok, width = attn_input.shape
    ct, rh = width // ROWB, width // ROWB // groups
    norm_factor = 2.0 / (tok * tiles * groups)
    dma = pltpu.SemaphoreType.DMA
    group = 4 * ROWB
    total = group * (2 * ROWB - 1)
    hess = pl.pallas_call(
        kernel,
        out_shape=[jax.ShapeDtypeStruct((rh, ct), jnp.float32)] * 2,
        in_specs=[pl.BlockSpec(memory_space=IN_SPACE)] * 2,
        out_specs=[pl.BlockSpec(memory_space=pltpu.VMEM)] * 2,
        scratch_shapes=[
            pltpu.VMEM((4 * (ROWB - 1), tok, ct), jnp.bfloat16),
            pltpu.VMEM((total, tok, ct), jnp.bfloat16),
            pltpu.VMEM((total, tok, ct), jnp.bfloat16),
            dma((2,)), dma((2, ROWB - 1)), dma((2, 2)), dma((total,)), dma((total,)),
            dma((2, ROWB - 1)), dma((2, groups, 2)), dma((2 * ROWB - 1, ROWB)), dma((2 * ROWB, ROWB)),
        ],
        compiler_params=pltpu.CompilerParams(collective_id=0, has_side_effects=True, vmem_limit_bytes=VMEM_LIMIT),
    )(pltpu.with_memory_space_constraint(attn_input, pltpu.HBM), pltpu.with_memory_space_constraint(mlp_input, pltpu.HBM))
    return hess[0][None] * norm_factor, hess[1][None] * norm_factor


def body(attn_input, mlp_input):
    if lax.axis_size("grp") == 2 and lax.axis_size("tile") == ROWB * ROWB:
        return fused(attn_input, mlp_input)
    return (hessian_share(attn_input), hessian_share(mlp_input))


def solution(mesh):
    in_specs = (P(("grp", "tile"), None), P(("grp", "tile"), None))
    out_specs = (P("tile", "grp", None), P("tile", "grp", None))
    return jax.shard_map(body, mesh=mesh, in_specs=in_specs, out_specs=out_specs, check_vma=False)
```

time: 94.7 us -> 89.2 us (0.942); the launches traced: 93.3 us -> 89.1 us
  Pallas kernels: 87.7 us -> 85.6 us
  local copies, waits for them, and re-layouts: 2.08 us -> 0 us
    pallas_call x1, Pallas kernels: 87.7 us -> 85.6 us  [fused(): pl.pallas_call(kernel, out_shape=[jax.ShapeDtypeStruct((rh, ct), jnp.floa...]
    unnamed x4 -> x0, local copies, waits for them, and re-layouts: 2.08 us -> none
where the time goes in v1:
time: 89.2 us; the launch traced here: 89.1 us
  Pallas kernels  85.6 us (96%)
  other arithmetic  2.85 us (3%)
    pallas_call x1, Pallas kernels, fused(): pl.pallas_call(kernel, out_shape=[jax.ShapeDtypeStruct((rh, ct), jnp.floa...  85.6 us
    mul x1, other arithmetic, fused(): return (hess[0][None] * norm_factor, hess[1][None] * norm_factor)  2.85 us

profile of v1, /device:TPU:3, one launch (start us, length us, event | category | flops | bytes accessed | tf_op | source)
XLA Modules:
  0.0 89.1 jit_solution(15249178919459754264)
XLA Ops:
  0.6 85.6 %shard_map.41 = (f32[512,1024]{1,0:T(8,128)S(1)}, f32[512,1024]{1,0:T(8,128)S(1)}) custom-call(bf16[64,4096]{1,0:T(8,128)(2,1)} %xa.1, bf16[64,4096]{1,0:T(8,128)(2,1)} %xm.1), custom_call_target="tpu_custom_call" | custom-call | tf_op jit(solution)/shard_map/pallas_call | solution.py:534
  86.2 2.9 %multiply_bitcast_fusion = (f32[1,512,1024]{2,1,0:T(8,128)}, f32[1,512,1024]{2,1,0:T(8,128)}) fusion(f32[512,1024]{1,0:T(8,128)S(1)} %get-tuple-element.5, f32[512,1024]{1,0:T(8,128)S(1)} %get-tuple-element.4), kind=kLoop, calls=%fused_computation | loop fusion | flops 1048576 | bytes 8388608 | tf_op jit(solution)/shard_map/mul | solution.py:548

commit v2 on v1

--- a/solution.py
+++ b/solution.py
@@ -11,12 +11,13 @@
 LINE = 0
 RING = 1
 AHEAD = 3
-CROSS_AT = 2
+CROSS_AT = 3
 CROSS_LATE = 9
-CROSS_WAIT = 5
+CROSS_WAIT = 7
 FAR_LAG = 1
-SPAN_LAG = 2
-MUL_LAG = 4
+SPAN_LAG = 3
+MUL_LAG = 5
+LATE_AT = 16
 VMEM_LIMIT = 48 * 1024 * 1024
 IN_SPACE = pltpu.HBM
 
@@ -423,6 +424,15 @@
                 def _():
                     turns(block, r, SPAN_LAG, row_turn(1, False))
 
+            if r == LATE_AT % planes:
+                @pl.when(slot_late & is_line & (block == LATE_AT // planes))
+                def _():
+                    for a in range(2):
+                        for gg in (LINE, RING):
+                            n = toward + own_index(a, place, gg)
+                            landed(cbuf.at[n], c_recv.at[n])
+                            pair_copy(n, d_send.at[toward // group, place]).start()
+
             at = r - MUL_LAG
             if (at - (planes - 1)) % planes == 0:
                 @pl.when(block == (planes - 1 - at) // planes)
@@ -449,13 +459,6 @@
 
     @pl.when(slot_late)
     def _():
-        for a in range(2):
-            @pl.when(is_line)
-            def _():
-                for gg in (LINE, RING):
-                    n = toward + own_index(a, place, gg)
-                    landed(cbuf.at[n], c_recv.at[n])
-                    pair_copy(n, d_send.at[toward // group, place]).start()
         for a in range(2):
             gather_waits(toward + own_index(a, 0, 0), False)
             product(a, toward + own_index(a, 0, 0), 2 * planes, rbuf)

time: 89.2 us -> 88.1 us (0.988)
  Pallas kernels: 85.6 us -> 84.5 us
    pallas_call x1, Pallas kernels: 85.6 us -> 84.5 us  [fused(): pl.pallas_call(kernel, out_shape=[jax.ShapeDtypeStruct((rh, ct), jnp.floa...]
where the time goes in v2:
time: 88.1 us; the launch traced here: 88 us
  Pallas kernels  84.5 us (96%)
  other arithmetic  2.85 us (3%)
    pallas_call x1, Pallas kernels, fused(): pl.pallas_call(kernel, out_shape=[jax.ShapeDtypeStruct((rh, ct), jnp.floa...  84.5 us
    mul x1, other arithmetic, fused(): return (hess[0][None] * norm_factor, hess[1][None] * norm_factor)  2.85 us

profile of v2, /device:TPU:3, one launch (start us, length us, event | category | flops | bytes accessed | tf_op | source)
XLA Modules:
  0.0 88.0 jit_solution(6970913832742904196)
XLA Ops:
  0.6 84.5 %shard_map.41 = (f32[512,1024]{1,0:T(8,128)S(1)}, f32[512,1024]{1,0:T(8,128)S(1)}) custom-call(bf16[64,4096]{1,0:T(8,128)(2,1)} %xa.1, bf16[64,4096]{1,0:T(8,128)(2,1)} %xm.1), custom_call_target="tpu_custom_call" | custom-call | tf_op jit(solution)/shard_map/pallas_call | solution.py:537
  85.1 2.9 %multiply_bitcast_fusion = (f32[1,512,1024]{2,1,0:T(8,128)}, f32[1,512,1024]{2,1,0:T(8,128)}) fusion(f32[512,1024]{1,0:T(8,128)S(1)} %get-tuple-element.5, f32[512,1024]{1,0:T(8,128)S(1)} %get-tuple-element.4), kind=kLoop, calls=%fused_computation | loop fusion | flops 1048576 | bytes 8388608 | tf_op jit(solution)/shard_map/mul | solution.py:551

commit v3 on v2

--- a/solution.py
+++ b/solution.py
@@ -69,7 +69,7 @@
     return jnp.where(turn == 0, home, jnp.where(turn == 1, near, jnp.where(turn == 2, far, ROWB - 1 - home)))
 
 
-def kernel(xa, xm, out_a, out_m, xbuf, cbuf, rbuf, own_sem, ld_sem, x_recv, c_recv, r_recv, s1_send, x_send, d_send, z_send):
+def kernel(xa, xm, out, xbuf, buf, own_sem, ld_sem, x_recv, c_recv, r_recv, s1_send, x_send, d_send, z_send, f_send):
     lines = planes = ROWB
     group = 4 * planes
     side = group * (lines - 1)
@@ -78,10 +78,10 @@
     t = lax.axis_index("tile")
     z, p = t // planes, t % planes
     tok, _ = xa.shape
-    ct = cbuf.shape[-1]
+    ct = buf.shape[-1]
+    cbuf, rbuf = buf.at[pl.ds(0, total)], buf.at[pl.ds(total, total)]
     rh = ct // 2
     xs = (xa, xm)
-    outs = (out_a, out_m)
     is_line = g == LINE
     line_half = pl.ds(LINE * rh, rh)
     my_half = pl.ds(pl.multiple_of(g * rh, rh), rh)
@@ -183,13 +183,15 @@
             greet(chip(z + 1, p, LINE))
 
         pl.semaphore_wait(
-            barrier, planes + jnp.where(z > 0, 1, 0) + jnp.where(z < lines - 1, 1, 0)
+            barrier, planes + 2 + jnp.where(z > 0, 1, 0) + jnp.where(z < lines - 1, 1, 0)
             + jnp.where(crosses(1), 1, 0) + jnp.where(crosses(2), 1, 0))
 
     @pl.when(~is_line)
     def _():
         for device in ring_next:
             greet(device)
+        for chip_next in (ring_fwd, ring_bwd):
+            greet(chip(z, chip_next, LINE))
         pl.semaphore_wait(barrier, planes + 2)
 
     def remote(src, dst, send_sem, recv_sem, device):
@@ -232,6 +234,15 @@
     def drain(count, sem, buf):
         ref = buf.at[pl.ds(0, count)]
         pltpu.make_async_copy(ref, ref, sem).wait()
+
+    def feed(sd, a, turn, gg):
+        way = (turn + gg) % 2
+        base = group * sd
+        to = base + own_index(a, next_turn(turn, way), gg)
+
+        @pl.when(is_root)
+        def _():
+            ring_copy(cbuf, base + own_index(a, turn, gg), to, way, f_send.at[sd, turn]).start()
 
     def col_turn(sd, turn, dist, near):
         for a in range(2):
@@ -259,21 +270,12 @@
                         main()
                     else:
                         pl.when(main_ok)(main)
+                    feed(sd, a, turn, gg)
                     if not (dist is None and turn == 0 and gg == RING):
                         pair_copy(n, d_send.at[sd, turn]).start()
 
                 if not (dist is None and turn == 0 and gg == LINE):
                     one()
-
-    def feed_turn(sd, turn, dist, near):
-        for a in range(2):
-            for gg in range(2):
-                n = group * sd + own_index(a, turn, gg)
-                if not (dist is None and turn == 0 and gg == RING):
-                    landed(cbuf.at[n], c_recv.at[n])
-                way = (turn + gg) % 2
-                to = group * sd + own_index(a, next_turn(turn, way), gg)
-                ring_copy(cbuf, n, to, way, z_send.at[sd, turn]).start()
 
     def row_turn(way, passes):
         def action(sd, turn, dist, near):
@@ -291,36 +293,29 @@
         return action
 
     def gather_waits(base, skip_own):
-        @pl.when(~is_root)
-        def _():
-            @pl.when(is_line)
-            def _():
-                for j in range(2 * planes):
-                    landed(rbuf.at[base + j, :, line_half], r_recv.at[base + j])
-
-            @pl.when(~is_line)
-            def _():
-                for j in range(2 * planes):
-                    if not (skip_own and j == RING):
-                        landed(cbuf.at[base + j], c_recv.at[base + j])
-
-    def product(a, base, count, rows):
-        lhs = rows[pl.ds(base, count), :, my_half].reshape(count * tok, rh)
-        rhs = cbuf[pl.ds(base, count)].reshape(count * tok, ct)
-        outs[a][...] += lax.dot_general(lhs, rhs, (((0,), (0,)), ((), ())), preferred_element_type=jnp.float32)
+        @pl.when(is_line & ~is_root)
+        def _():
+            for j in range(2 * planes):
+                landed(rbuf.at[base + j, :, line_half], r_recv.at[base + j])
+
+        @pl.when(~is_line)
+        def _():
+            for j in range(2 * planes):
+                if not (skip_own and j == RING):
+                    landed(cbuf.at[base + j], c_recv.at[base + j])
+
+    rows_from = jnp.where(is_root, 0, total)
 
     def multiply(sd, skip_own=False):
-        for a in range(2):
+        def one(a, carry):
             base = group * sd + own_index(a, 0, 0)
             gather_waits(base, skip_own)
-
-            @pl.when(is_root)
-            def _():
-                product(a, base, 2 * planes, cbuf)
-
-            @pl.when(~is_root)
-            def _():
-                product(a, base, 2 * planes, rbuf)
+            lhs = buf[pl.ds(base + rows_from, 2 * planes), :, my_half].reshape(2 * planes * tok, rh)
+            rhs = buf[pl.ds(base, 2 * planes)].reshape(2 * planes * tok, ct)
+            out[a] += lax.dot_general(lhs, rhs, (((0,), (0,)), ((), ())), preferred_element_type=jnp.float32)
+            return carry
+
+        lax.fori_loop(0, 2, one, 0)
 
     for a in range(2):
         load_own(a).wait()
@@ -333,6 +328,7 @@
             def _():
                 line_copy(n, n + toward, z + end_step, z_send.at[0, 0]).start()
             line_copy(n, n + away, z - end_step, z_send.at[2 * lines - 1, 0]).start()
+            feed(0, a, 0, LINE)
             pair_copy(n, d_send.at[0, 0]).start()
 
         @pl.when(~is_line)
@@ -348,8 +344,8 @@
         def _():
             for a in range(2):
                 lend_copy(a, turn).start()
-    for out in outs:
-        out[...] = jnp.zeros_like(out)
+    for a in range(2):
+        out[a] = jnp.zeros_like(out[a])
 
     def send_cross(a, turn):
         cross_copy(a, turn, LINE).start()
@@ -402,10 +398,6 @@
                                 send_cross(a, turn)
                 turns(block, r, 0, col_turn)
 
-            @pl.when(~is_line & is_root)
-            def _():
-                turns(block, r, 0, feed_turn)
-
             @pl.when(~is_line & ~is_root)
             def _():
                 @pl.when(fwd < planes - 1)
@@ -457,12 +449,6 @@
     steps = planes * lines - AHEAD + FAR_LAG + MUL_LAG
     lax.fori_loop(0, (steps + planes - 1) // planes, block_steps, 0)
 
-    @pl.when(slot_late)
-    def _():
-        for a in range(2):
-            gather_waits(toward + own_index(a, 0, 0), False)
-            product(a, toward + own_index(a, 0, 0), 2 * planes, rbuf)
-
     def done(j, carry):
         dist = j % lines
         near = j < lines
@@ -473,6 +459,10 @@
             for turn in range(planes):
                 @pl.when(is_line)
                 def _():
+                    @pl.when(is_root)
+                    def _():
+                        drain(4, f_send.at[sd, turn], cbuf)
+
                     @pl.when(jnp.logical_not(near) | (~at_end & ~((dist == 0) & crosses(turn))))
                     def _():
                         drain(4, z_send.at[sd, turn], cbuf)
@@ -493,7 +483,7 @@
 
                 @pl.when(~is_line)
                 def _():
-                    @pl.when(is_root | (fwd == 2))
+                    @pl.when(fwd == 2)
                     def _():
                         drain(4, z_send.at[sd, turn], cbuf)
 
@@ -524,6 +514,10 @@
             @pl.when(~is_line & ~at_end & crosses(turn))
             def _():
                 lend_copy(a, turn).wait_send()
+
+    @pl.when(slot_late)
+    def _():
+        multiply(toward // group)
 
 
 def fused(attn_input, mlp_input):
@@ -536,15 +530,15 @@
     total = group * (2 * ROWB - 1)
     hess = pl.pallas_call(
         kernel,
-        out_shape=[jax.ShapeDtypeStruct((rh, ct), jnp.float32)] * 2,
+        out_shape=jax.ShapeDtypeStruct((2, rh, ct), jnp.float32),
         in_specs=[pl.BlockSpec(memory_space=IN_SPACE)] * 2,
-        out_specs=[pl.BlockSpec(memory_space=pltpu.VMEM)] * 2,
+        out_specs=pl.BlockSpec(memory_space=pltpu.VMEM),
         scratch_shapes=[
             pltpu.VMEM((4 * (ROWB - 1), tok, ct), jnp.bfloat16),
-            pltpu.VMEM((total, tok, ct), jnp.bfloat16),
-            pltpu.VMEM((total, tok, ct), jnp.bfloat16),
+            pltpu.VMEM((2 * total, tok, ct), jnp.bfloat16),
             dma((2,)), dma((2, ROWB - 1)), dma((2, 2)), dma((total,)), dma((total,)),
             dma((2, ROWB - 1)), dma((2, groups, 2)), dma((2 * ROWB - 1, ROWB)), dma((2 * ROWB, ROWB)),
+            dma((2 * ROWB - 1, ROWB)),
         ],
         compiler_params=pltpu.CompilerParams(collective_id=0, has_side_effects=True, vmem_limit_bytes=VMEM_LIMIT),
     )(pltpu.with_memory_space_constraint(attn_input, pltpu.HBM), pltpu.with_memory_space_constraint(mlp_input, pltpu.HBM))

time: 88.1 us -> 88 us (level)
  no operation moved by 1% of the time
where the time goes in v3:
time: 88 us; the launch traced here: 87.8 us
  Pallas kernels  84.3 us (96%)
  other arithmetic  2.85 us (3%)
    pallas_call x1, Pallas kernels, fused(): pl.pallas_call(kernel, out_shape=jax.ShapeDtypeStruct((2, rh, ct), jnp.fl...  84.3 us
    mul x1, other arithmetic, fused(): return (hess[0][None] * norm_factor, hess[1][None] * norm_factor)  2.85 us

profile of v3, /device:TPU:3, one launch (start us, length us, event | category | flops | bytes accessed | tf_op | source)
XLA Modules:
  0.0 87.8 jit_solution(913237194530963810)
XLA Ops:
  0.6 84.3 %shard_map.41 = f32[2,512,1024]{2,1,0:T(8,128)S(1)} custom-call(bf16[64,4096]{1,0:T(8,128)(2,1)} %xa.1, bf16[64,4096]{1,0:T(8,128)(2,1)} %xm.1), custom_call_target="tpu_custom_call" | custom-call | tf_op jit(solution)/shard_map/pallas_call | solution.py:531
  85.0 2.9 %slice_multiply_fusion = (f32[1,512,1024]{2,1,0:T(8,128)}, f32[1,512,1024]{2,1,0:T(8,128)}) fusion(f32[2,512,1024]{2,1,0:T(8,128)S(1)} %shard_map.41), kind=kLoop, calls=%fused_computation | loop fusion | flops 1048576 | bytes 8388608 | tf_op jit(solution)/shard_map/mul | solution.py:545

commit v4 on v3

--- a/solution.py
+++ b/solution.py
@@ -11,13 +11,13 @@
 LINE = 0
 RING = 1
 AHEAD = 3
-CROSS_AT = 3
+CROSS_AT = 4
 CROSS_LATE = 9
-CROSS_WAIT = 7
+CROSS_WAIT = 8
 FAR_LAG = 1
-SPAN_LAG = 3
-MUL_LAG = 5
-LATE_AT = 16
+SPAN_LAG = 4
+MUL_LAG = 6
+LATE_AT = 17
 VMEM_LIMIT = 48 * 1024 * 1024
 IN_SPACE = pltpu.HBM
 

time: 88 us -> 87.6 us (level)
  no operation moved by 1% of the time
where the time goes in v4:
time: 87.6 us; the launch traced here: 87.4 us
  Pallas kernels  84 us (96%)
  other arithmetic  2.85 us (3%)
    pallas_call x1, Pallas kernels, fused(): pl.pallas_call(kernel, out_shape=jax.ShapeDtypeStruct((2, rh, ct), jnp.fl...  84 us
    mul x1, other arithmetic, fused(): return (hess[0][None] * norm_factor, hess[1][None] * norm_factor)  2.85 us

profile of v4, /device:TPU:3, one launch (start us, length us, event | category | flops | bytes accessed | tf_op | source)
XLA Modules:
  0.0 87.4 jit_solution(12019376201550813910)
XLA Ops:
  0.6 84.0 %shard_map.41 = f32[2,512,1024]{2,1,0:T(8,128)S(1)} custom-call(bf16[64,4096]{1,0:T(8,128)(2,1)} %xa.1, bf16[64,4096]{1,0:T(8,128)(2,1)} %xm.1), custom_call_target="tpu_custom_call" | custom-call | tf_op jit(solution)/shard_map/pallas_call | solution.py:531
  84.6 2.9 %slice_multiply_fusion = (f32[1,512,1024]{2,1,0:T(8,128)}, f32[1,512,1024]{2,1,0:T(8,128)}) fusion(f32[2,512,1024]{2,1,0:T(8,128)S(1)} %shard_map.41), kind=kLoop, calls=%fused_computation | loop fusion | flops 1048576 | bytes 8388608 | tf_op jit(solution)/shard_map/mul | solution.py:545
